TPU v7x, 32 devices: a whole 2x2x4 slice. The times are simulated.
32 devices in a mesh: row: 2 (over y), phi: 16 (over z, x, core).
Axes of the slice: x: 2, y: 2, z: 4, core: 2. Of those that a mesh axis runs over, the one named last changes fastest.
Arguments:
- density: float32 [32, 2048, 512], P('row', 'phi'), may hold values from 0.3 to 3
- velocity: float32 [3, 32, 2048, 512], P(None, 'row', 'phi'), may hold values from -3 to 3
- magnetic: float32 [3, 32, 2048, 512], P(None, 'row', 'phi'), may hold values from -6 to 6
Outputs:
- density_next: float32 [32, 2048, 512], P('row', 'phi')
- magnetic_next: float32 [3, 32, 2048, 512], P(None, 'row', 'phi')
All inputs are finite; a program needn't handle non-finite values.
Results may differ from a plain program's by a relative error of at most 0.0003.
Values sent between devices are 32-bit elements; how exact they have to be, the bound alone decides.
A program may use at most 256 MiB of HBM per device.

v0:
```python
from functools import partial

import jax
import jax.numpy as jnp
from jax import lax
from jax.sharding import PartitionSpec as P

NP = 2048
NPOL = 128


COURANT_RAD = 0.3
COURANT_POL = 0.25
COURANT_AZI = 0.35
SOUND_SPEED = 1.0


def extended(value, sides, width, wrap):
    for axis, dim in sides:
        devices, length = (lax.axis_size(axis), value.shape[dim])
        up = [(i, (i + 1) % devices) for i in range(devices if wrap else devices - 1)]
        down = [(j, i) for i, j in up]
        last = lax.slice_in_dim(value, length - width, length, axis=dim)
        leading = lax.slice_in_dim(value, 0, width, axis=dim)
        before = lax.ppermute(last, axis, up)
        after = lax.ppermute(leading, axis, down)
        value = jnp.concatenate([before, value, after], axis=dim)
    return value


def shift_theta(values, offset):
    if offset == 0:
        return values
    if offset > 0:
        border = jnp.repeat(values[..., -1:], offset, axis=-1)
        return jnp.concatenate([values[..., offset:], border], axis=-1)
    border = jnp.repeat(values[..., :1], -offset, axis=-1)
    return jnp.concatenate([border, values[..., :offset]], axis=-1)


def interface_value(outer_left, inner_left, inner_right, outer_right):
    guess = 7.0 / 12.0 * (inner_left + inner_right) - 1.0 / 12.0 * (outer_left + outer_right)
    return jnp.clip(
        guess, jnp.minimum(inner_left, inner_right), jnp.maximum(inner_left, inner_right)
    )


def edge_values(nearby):
    centre = nearby(0)
    left_face = interface_value(nearby(-2), nearby(-1), centre, nearby(1))
    right_face = interface_value(nearby(-1), centre, nearby(1), nearby(2))
    to_left = left_face - centre
    to_right = right_face - centre
    left_limited = jnp.clip(to_left, -2.0 * jnp.abs(to_right), 2.0 * jnp.abs(to_right))
    right_limited = jnp.clip(to_right, -2.0 * jnp.abs(to_left), 2.0 * jnp.abs(to_left))
    return (centre + left_limited, centre + right_limited)


def hll_flux(dens_left, dens_right, speed_left, speed_right):
    slowest = jnp.minimum(jnp.minimum(speed_left, speed_right) - SOUND_SPEED, 0.0)
    fastest = jnp.maximum(jnp.maximum(speed_left, speed_right) + SOUND_SPEED, 0.0)
    upwind = fastest * dens_left * speed_left - slowest * dens_right * speed_right
    return (upwind + slowest * fastest * (dens_right - dens_left)) / (fastest - slowest)


def axis_divergence(dens, speed, axis, count, ghost):

    def picker(field):

        def nearby(offset):
            return lax.slice_in_dim(
                field, ghost - 1 + offset, ghost + 1 + offset + count, axis=axis
            )

        return nearby

    def window(values, start, stop):
        return lax.slice_in_dim(values, start, stop, axis=axis)

    dens_left, dens_right = edge_values(picker(dens))
    speed_left, speed_right = edge_values(picker(speed))
    flux = hll_flux(
        window(dens_right, 0, count + 1),
        window(dens_left, 1, count + 2),
        window(speed_right, 0, count + 1),
        window(speed_left, 1, count + 2),
    )
    return window(flux, 1, count + 1) - window(flux, 0, count)


def theta_divergence(dens, speed):
    dens_left, dens_right = edge_values(partial(shift_theta, dens))
    speed_left, speed_right = edge_values(partial(shift_theta, speed))
    flux = hll_flux(
        shift_theta(dens_right, -1), dens_left, shift_theta(speed_right, -1), speed_left
    )
    position = lax.broadcasted_iota(jnp.int32, flux.shape, flux.ndim - 1)
    flux = jnp.where(position == 0, jnp.zeros_like(flux), flux)
    upper_flux = jnp.concatenate([flux[..., 1:], jnp.zeros_like(flux[..., :1])], axis=-1)
    return upper_flux - flux


def advance(primitive, magnetic, ghost, face_ghost, radial, azimuth):
    dens = primitive[0]
    radial_speed = primitive[1]
    polar_speed = primitive[2]
    azimuth_speed = primitive[3]

    def inner(values, width):
        return values[width : width + radial, width : width + azimuth]

    def box(values, width):
        return values[width - 1 : width + radial + 1, width - 1 : width + azimuth + 1]

    rad_term = axis_divergence(
        dens[:, ghost : ghost + azimuth], radial_speed[:, ghost : ghost + azimuth], 0, radial, ghost
    )
    azi_term = axis_divergence(
        dens[ghost : ghost + radial], azimuth_speed[ghost : ghost + radial], 1, azimuth, ghost
    )
    dens_inner = inner(dens, ghost)
    pol_term = theta_divergence(dens_inner, inner(polar_speed, ghost))
    density_next = (
        dens_inner - COURANT_RAD * rad_term - COURANT_POL * pol_term - COURANT_AZI * azi_term
    )
    radial_span = magnetic[0][
        face_ghost - 1 : face_ghost + radial + 2, face_ghost - 1 : face_ghost + azimuth + 1
    ]
    radial_cell = 0.5 * (radial_span[:-1] + radial_span[1:])
    azimuth_span = magnetic[2][
        face_ghost - 1 : face_ghost + radial + 1, face_ghost - 1 : face_ghost + azimuth + 2
    ]
    azimuth_cell = 0.5 * (azimuth_span[:, :-1] + azimuth_span[:, 1:])
    polar_box = box(magnetic[1], face_ghost)
    polar_cell = 0.5 * (polar_box + shift_theta(polar_box, 1))
    speed_r = box(radial_speed, ghost)
    speed_t = box(polar_speed, ghost)
    speed_p = box(azimuth_speed, ghost)
    radial_emf = -(speed_t * azimuth_cell - speed_p * polar_cell)
    polar_emf = -(speed_p * radial_cell - speed_r * azimuth_cell)
    azimuth_emf = -(speed_r * polar_cell - speed_t * radial_cell)
    radial_edge = 0.5 * (radial_emf[1 : radial + 1, :-1] + radial_emf[1 : radial + 1, 1:])
    radial_below = 0.5 * (shift_theta(radial_edge, -1) + radial_edge)
    radial_above = 0.5 * (radial_edge + shift_theta(radial_edge, 1))
    azimuth_edge = 0.5 * (azimuth_emf[:-1, 1 : azimuth + 1] + azimuth_emf[1:, 1 : azimuth + 1])
    azimuth_below = 0.5 * (shift_theta(azimuth_edge, -1) + azimuth_edge)
    azimuth_above = 0.5 * (azimuth_edge + shift_theta(azimuth_edge, 1))
    polar_edge = 0.25 * (
        polar_emf[:-1, :-1] + polar_emf[1:, :-1] + polar_emf[:-1, 1:] + polar_emf[1:, 1:]
    )
    radial_next = (
        inner(magnetic[0], face_ghost)
        - COURANT_POL * (azimuth_above[:radial] - azimuth_below[:radial])
        + COURANT_AZI * (polar_edge[:radial, 1:] - polar_edge[:radial, :-1])
    )
    polar_next = (
        inner(magnetic[1], face_ghost)
        - COURANT_AZI * (radial_below[:, 1:] - radial_below[:, :-1])
        + COURANT_RAD * (azimuth_below[1:] - azimuth_below[:-1])
    )
    azimuth_next = (
        inner(magnetic[2], face_ghost)
        - COURANT_RAD * (polar_edge[1:, :azimuth] - polar_edge[:-1, :azimuth])
        + COURANT_POL * (radial_above[:, :azimuth] - radial_below[:, :azimuth])
    )
    return (density_next, jnp.stack([radial_next, polar_next, azimuth_next]))


def radial_fix(padded, width):
    first_row = lax.axis_index("row") == 0
    last_row = lax.axis_index("row") == lax.axis_size("row") - 1
    inner_low = jnp.broadcast_to(padded[:, width : width + 1], padded[:, :width].shape)
    inner_high = jnp.broadcast_to(padded[:, -width - 1 : -width], padded[:, -width:].shape)
    low_side = jnp.where(first_row, inner_low, padded[:, :width])
    high_side = jnp.where(last_row, inner_high, padded[:, -width:])
    return jnp.concatenate([low_side, padded[:, width:-width], high_side], axis=1)


def ghost_state(values):
    padded = radial_fix(extended(values, (("row", 1),), 3, False), 3)
    result = extended(padded, (("phi", 2),), 3, True)
    return result


def per_device(density, velocity, magnetic):
    radial, azimuth, theta_count = density.shape
    half_polar = NPOL // 2
    primitive = jnp.concatenate([density[None], velocity], axis=0)
    polar_rows = jnp.concatenate(
        [primitive[..., :half_polar], primitive[..., theta_count - half_polar :]], axis=-1
    )
    polar_rows = jnp.swapaxes(polar_rows, 2, 3)
    column = lax.broadcasted_iota(jnp.int32, (NP, NP), 1)
    sample = lax.broadcasted_iota(jnp.int32, (NP, NP), 0)
    mode_index = jnp.where(column <= NP // 2, column, column - NP // 2)
    phase_angle = (sample * mode_index % NP).astype(jnp.float32) * (2.0 * jnp.pi / NP)
    fourier_basis = jnp.where(column <= NP // 2, jnp.cos(phase_angle), jnp.sin(phase_angle))
    mode_row = mode_index[0]
    column_row = column[0]
    weights = jnp.where((mode_row == 0) | (column_row == NP // 2), 1.0 / NP, 2.0 / NP).astype(
        jnp.float32
    )
    mode_sine = jnp.sin(jnp.pi * mode_row.astype(jnp.float32) / NP)
    edge_sine = jnp.sin(jnp.pi * (half_polar + 0.5) / theta_count)
    lines = lax.all_to_all(polar_rows, "phi", split_axis=2, concat_axis=3, tiled=True)
    local_rows = lines.shape[2]
    global_row = lax.axis_index("phi") * local_rows + jnp.arange(local_rows, dtype=jnp.int32)
    theta_row = jnp.where(global_row < half_polar, global_row, theta_count - NPOL + global_row)
    row_sine = jnp.sin(jnp.pi * (theta_row.astype(jnp.float32) + 0.5) / theta_count)
    row_square = (row_sine * row_sine)[:, None]
    mode_square = (edge_sine * mode_sine)[None, :]
    damping = row_square / jnp.maximum(row_square, mode_square * mode_square)
    spectrum = jnp.dot(
        lines.reshape(-1, NP),
        fourier_basis,
        precision=lax.Precision.HIGHEST,
        preferred_element_type=jnp.float32,
    ).reshape(lines.shape)
    spectrum = spectrum * (damping * weights[None, :])
    smoothed = lax.dot_general(
        spectrum.reshape(-1, NP),
        fourier_basis,
        (((1,), (1,)), ((), ())),
        precision=lax.Precision.HIGHEST,
        preferred_element_type=jnp.float32,
    ).reshape(lines.shape)
    returned = lax.all_to_all(smoothed, "phi", split_axis=3, concat_axis=2, tiled=True)
    returned = jnp.swapaxes(returned, 2, 3)
    primitive = jnp.concatenate(
        [
            returned[..., :half_polar],
            primitive[..., half_polar : theta_count - half_polar],
            returned[..., half_polar:],
        ],
        axis=-1,
    )
    state = ghost_state(jnp.concatenate([primitive, magnetic], axis=0))
    primitive_padded = state[:4]
    magnetic_padded = state[4:]
    face_ghost = 3
    return advance(primitive_padded, magnetic_padded, 3, face_ghost, radial, azimuth)


def solution(mesh):
    placed = (P("row", "phi", None), P(None, "row", "phi", None), P(None, "row", "phi", None))
    return jax.shard_map(
        per_device,
        mesh=mesh,
        in_specs=placed,
        out_specs=(P("row", "phi", None), P(None, "row", "phi", None)),
        check_vma=False,
    )
```

profile of v0, /device:TPU:13, one launch (start us, length us, event | category | flops | bytes accessed | tf_op | source)
XLA Modules:
  0.0 1016.8 jit_solution(8713738832390552506)
XLA Ops:
  0.6 5.4 fusion.88
  6.0 5.4 copy.106
  11.4 6.5 all-to-all-start
  18.1 2.1 iota_select_fusion
  20.5 67.5 %fusion.152 = f32[2048,2048,1,1]{1,0,3,2:T(8,128)} fusion(s32[2048]{0:T(1024)S(1)} %iota_add_fusion, pred[2048]{0:T(1024)(128)(4,1)S(1)} %iota_compare_fusion.2), kind=kLoop, calls=%fused_computation.10.clone.1 | loop fusion | flops 67108864 | bytes 16787456 | tf_op jit(solution)/shard_map/dot_general | solution.py:213
  88.0 20.2 %all-to-all-done = f32[4,16,128,128]{3,1,0,2:T(8,128)} async-done(((f32[4,16,128,128]{3,1,0,2:T(8,128)}), f32[4,16,128,128]{3,1,0,2:T(8,128)}, u32[]{:S(2)}, u32[]{:S(2)}) %all-to-all-start) | async-done | bytes 4194336 | tf_op jit(solution)/shard_map/all_to_all | solution.py:205
  108.2 34.1 %fusion.5 = f32[4,16,8,2048]{3,2,1,0:T(8,128)S(1)} fusion(f32[4,16,128,128]{3,1,0,2:T(8,128)} %all-to-all-done, f32[2048,2048,1,1]{1,0,3,2:T(8,128)} %fusion.152), kind=kOutput, calls=%fused_computation.9 | convolution fusion | flops 25769803776 | bytes 25165824 | tf_op jit(solution)/shard_map/dot_general | solution.py:213
  142.6 94.4 %fusion.3 = f32[4,16,8,2048]{3,2,1,0:T(8,128)} fusion(pred[2048]{0:T(1024)(128)(4,1)S(1)} %iota_compare_fusion.2, s32[2048]{0:T(1024)S(1)} %iota_add_fusion, f32[4,16,8,2048]{3,2,1,0:T(8,128)S(1)} %fusion.150), kind=kOutput, calls=%fused_computation.7 | convolution fusion | flops 25836912640 | bytes 8398848 | tf_op jit(solution)/shard_map/dot_general | solution.py:220
  237.0 26.4 %copy.108 = f32[4,16,8,2048]{1,2,0,3:T(8,128)} copy(f32[4,16,8,2048]{3,2,1,0:T(8,128)} %fusion.3) | data formatting | bytes 8388608 | tf_op jit(solution)/shard_map/dot_general | solution.py:220
  263.4 22.0 %reshape.119 = f32[16,1,65536]{2,1,0:T(1,128)} reshape(f32[2048,4,8,16]{3,2,1,0:T(8,128)} %bitcast.95) | data formatting | bytes 8388608
  285.4 7.0 all-to-all-start.1
  292.4 11.6 %pad_maximum_fusion.1 = f32[4,16,128,384]{3,2,0,1:T(8,128)} fusion(f32[1,16,128,512]{3,2,0,1:T(8,128)} %bitcast.114, f32[3,16,128,512]{3,2,1,0:T(8,128)} %param.4), kind=kLoop, calls=%fused_computation.13 | loop fusion | flops 3145728 | bytes 29360128 | tf_op jit(solution)/shard_map/concatenate | solution.py:188
  304.0 78.6 %all-to-all-done.1 = f32[16,1,65536]{2,1,0:T(1,128)} async-done(((f32[16,1,65536]{2,1,0:T(1,128)}), f32[16,1,65536]{2,1,0:T(1,128)}, u32[]{:S(2)}, u32[]{:S(2)}) %all-to-all-start.1) | async-done | bytes 4194336 | tf_op jit(solution)/shard_map/all_to_all | solution.py:227
  383.1 13.7 %reduce.8 = f32[16,65536]{1,0:T(8,128)} reduce(f32[16,1,65536]{2,1,0:T(1,128)} %all-to-all-done.1, f32[]{:T(128)} %broadcast.356), dimensions={1}, to_apply=%all_to_all.27.reduce_sub_computation | reduce | bytes 8388612 | tf_op jit(solution)/shard_map/all_to_all | solution.py:227
  396.8 25.8 %reshape.120 = f32[2048,4,8,16]{3,2,1,0:T(8,128)} reshape(f32[16,65536]{1,0:T(8,128)} %reduce.8) | data formatting | bytes 8388608
  422.6 21.1 %copy.110 = f32[4,16,16,8,128]{4,3,2,1,0:T(8,128)} copy(f32[4,16,16,8,128]{1,3,0,4,2:T(8,128)} %bitcast.96) | data formatting | bytes 8388608 | tf_op jit(solution)/shard_map/all_to_all | solution.py:227
  443.8 4.0 fusion.134
  447.8 3.8 copy.112
  451.6 2.8 copy.111
  454.4 6.3 pad_maximum_fusion.6
  460.7 3.3 copy.116
  464.0 4.6 collective-permute-start.1
  468.6 3.2 copy.114
  473.2 4.2 maximum_bitcast_fusion.1
  477.4 106.1 %collective-permute-done.1 = f32[7,3,128,512]{3,2,1,0:T(8,128)} collective-permute-done((f32[7,3,128,512]{3,2,1,0:T(8,128)}, f32[7,3,128,512]{3,2,1,0:T(8,128)}, u32[]{:S(2)}, u32[]{:S(2)}) %collective-permute-start.1) | collective-permute-done | bytes 5505056 | tf_op jit(solution)/shard_map/ppermute | solution.py:26
  583.5 3.6 copy_select_fusion
  587.1 5.9 collective-permute-done
  593.1 7.3 copy_select_fusion.1
  601.8 2.9 pad_maximum_fusion.20
  605.0 2.2 collective-permute-start.3
  607.5 3.4 collective-permute-start.2
  611.4 21.4 %collective-permute-done.3 = f32[7,22,3,512]{3,1,2,0:T(8,128)S(1)} collective-permute-done((f32[7,22,3,512]{3,1,2,0:T(8,128)S(1)}, f32[7,22,3,512]{3,1,2,0:T(8,128)S(1)}, u32[]{:S(2)}, u32[]{:S(2)}) %collective-permute-start.3) | collective-permute-done | bytes 946208 | tf_op jit(solution)/shard_map/ppermute | solution.py:26
  636.2 57.4 %pad_maximum_fusion = f32[7,22,134,512]{3,2,0,1:T(8,128)} fusion(f32[7,22,3,512]{3,2,0,1:T(4,128)} %copy.121, f32[7,3,128,512]{3,2,0,1:T(8,128)} %copy-done.6, f32[4,16,128,64]{3,2,0,1:T(8,128)S(1)} %copy-done.2, f32[4,16,128,384]{3,2,0,1:T(8,128)S(1)} %bitcast.86, f32[4,16,128,64]{3,2,0,1:T(8,128)} %copy.111, f32[7,3,128,512]{3,2,0,1:T(8,128)} %copy_select_fusion.1, ...), kind=kLoop, calls=%fused_computation | loop fusion | flops 73959424 | bytes 84525056 | tf_op jit(solution)/shard_map/concatenate | solution.py:27
  693.7 8.2 slice_bitcast_fusion.8
  701.9 25.3 %slice_bitcast_fusion.3 = (f32[22,134,512]{2,1,0:T(8,128)}, f32[22,134,512]{2,1,0:T(8,128)}, f32[22,134,512]{2,1,0:T(8,128)S(1)}, f32[22,134,512]{2,1,0:T(8,128)...) fusion(f32[7,22,134,512]{3,2,0,1:T(8,128)} %pad_maximum_fusion), kind=kLoop, calls=%fused_computation.18 | loop fusion | bytes 84525056 | tf_op jit(solution)/shard_map/squeeze | solution.py:152
  727.2 2.3 slice_reduce_fusion.1
  729.5 5.4 fusion.129
  734.9 5.3 fusion.128
  740.2 2.0 slice_reduce_fusion.3
  742.2 5.3 fusion.127
  747.4 5.3 fusion.126
  753.1 4.4 slice.612
  757.5 27.9 %fusion.15 = (f32[18,128,512]{2,1,0:T(8,128)}, f32[18,128,512]{2,1,0:T(8,128)}, f32[18,128,512]{2,1,0:T(8,128)}, f32[18,128,512]{2,1,0:T(8,128)}, f32[18,128,512]{2,1,0:T(8,128)}, /*index=5*/f32[18,128,512]{2,1,0:T(8,128)}) fusion(f32[22,134,512]{2,1,0:T(8,128)} %copy-done, f32[22,134,512]{2,1,0:T(8,128)} %get-tuple-element.21), kind=kLoop, calls=%fused_computation.46 | loop fusion | flops 47185920 | bytes 75497472 | tf_op jit(solution)/shard_map/sub | solution.py:53
  785.4 15.4 %subtract_negate_fusion.1 = f32[18,130,512]{2,1,0:T(8,128)} fusion(f32[22,134,512]{2,1,0:T(8,128)} %get-tuple-element.24, f32[22,134,512]{2,1,0:T(8,128)} %get-tuple-element.21, f32[22,134,512]{2,1,0:T(8,128)} %get-tuple-element.18, f32[22,134,512]{2,1,0:T(8,128)} %get-tuple-element.23), kind=kLoop, calls=%fused_computation.35 | loop fusion | flops 9584640 | bytes 33546240 | tf_op jit(solution)/shard_map/neg | solution.py:140
  800.8 23.7 %subtract_negate_fusion.2 = (f32[18,130,512]{2,1,0:T(8,128)}, f32[18,130,512]{2,1,0:T(8,128)}) fusion(f32[22,134,512]{2,1,0:T(8,128)} %copy-done.1, f32[22,134,512]{2,1,0:T(8,128)} %get-tuple-element.21, f32[22,134,512]{2,1,0:T(8,128)} %get-tuple-element.18, f32[18,130,1]{2,1,0:T(8,128)S(1)} %slice.613, f32[18,130,511]{2,1,0:T(8,128)} %slice.612, ...), kind=kLoop, calls=%fused_computation.36 | loop fusion | flops 17971200 | bytes 52715520 | tf_op jit(solution)/shard_map/neg | solution.py:141
  824.4 5.0 fusion.32
  829.5 1.8 fusion.131
  831.2 5.0 fusion.130
  836.9 5.8 fusion.133
  849.1 16.7 %minimum_add_fusion = (f32[16,128,512]{2,1,0:T(8,128)}, f32[16,128,512]{2,1,0:T(8,128)}) fusion(f32[16,128,2]{2,1,0:T(8,128)S(1)} %reshape.113, f32[16,128,510]{2,1,0:T(8,128)S(1)} %copy-done.9, f32[16,128,510]{2,1,0:T(8,128)S(1)} %copy-done.7, f32[16,128,2]{2,1,0:T(8,128)S(1)} %reshape.112, f32[22,134,512]{2,1,0:T(8,128)S(1)} %bitcast.84, ...), kind=kLoop, calls=%fused_computation.206 | loop fusion | flops 62914560 | bytes 50331648 | tf_op jit(solution)/shard_map/add | solution.py:56
  865.8 2.5 slice.578
  868.3 2.3 slice.570
  870.6 21.0 %divide_select_fusion = f32[16,128,512]{2,1,0:T(8,128)} fusion(f32[16,128,511]{2,1,0:T(8,128)} %bitcast.111, f32[16,128,1]{2,1,0:T(8,128)} %slice.578, f32[16,128,2]{2,1,0:T(8,128)S(1)} %reshape.113, f32[16,128,510]{2,1,0:T(8,128)} %get-tuple-element.46, f32[16,128,510]{2,1,0:T(8,128)S(1)} %copy-done.8, f32[16,128,2]{2,1,0:T(8,128)S(1)} %reshape.112, ...), kind=kLoop, calls=%fused_computation.205 | loop fusion | flops 83886080 | bytes 54526464 | tf_op jit(solution)/shard_map/jit(_where)/select_n | solution.py:98
  891.6 5.5 slice.580
  897.1 9.5 fusion.10
  906.7 11.6 %fusion.39 = (f32[16,130,512]{2,1,0:T(8,128)}, f32[16,130,512]{2,1,0:T(8,128)}, f32[16,130,512]{2,1,0:T(8,128)}, f32[16,130,512]{2,1,0:T(8,128)}, f32[16,130,512]{2,1,0:T(8,128)}, /*index=5*/f32[16,130,512]{2,1,0:T(8,128)}) fusion(f32[16,134,512]{2,1,0:T(8,128)S(1)} %bitcast.92, f32[16,134,512]{2,1,0:T(8,128)S(1)} %bitcast.90), kind=kLoop, calls=%fused_computation.82 | loop fusion | flops 42598400 | bytes 68157440 | tf_op jit(solution)/shard_map/sub | solution.py:53
  918.3 5.4 fusion.61
  923.7 4.9 fusion.62
  928.6 1.8 slice-done.23
  931.7 16.6 %subtract_divide_fusion = f32[16,129,512]{2,1,0:T(8,128)} fusion(f32[16,130,512]{2,1,0:T(8,128)S(1)} %bitcast.108, f32[16,130,512]{2,1,0:T(8,128)S(1)} %bitcast.110, f32[16,130,512]{2,1,0:T(8,128)S(1)} %bitcast.106, f32[16,130,512]{2,1,0:T(8,128)} %get-tuple-element.73, f32[16,130,512]{2,1,0:T(8,128)} %get-tuple-element.72, ...), kind=kLoop, calls=%fused_computation.131 | loop fusion | flops 43327488 | bytes 54951936 | tf_op jit(solution)/shard_map/div | solution.py:63
  948.2 20.9 %subtract_divide_fusion.1 = f32[17,128,512]{2,1,0:T(8,128)} fusion(f32[18,128,512]{2,1,0:T(8,128)} %get-tuple-element.51, f32[18,128,512]{2,1,0:T(8,128)} %get-tuple-element.52, f32[18,128,512]{2,1,0:T(8,128)} %get-tuple-element.50, f32[18,128,512]{2,1,0:T(8,128)} %get-tuple-element.76, f32[18,128,512]{2,1,0:T(8,128)} %get-tuple-element.75, ...), kind=kLoop, calls=%fused_computation.132 | loop fusion | flops 45678592 | bytes 57933824 | tf_op jit(solution)/shard_map/div | solution.py:63
  969.2 10.8 %fusion.83 = f32[16,128,512]{2,1,0:T(8,128)} fusion(f32[16,129,512]{2,1,0:T(8,128)} %subtract_divide_fusion, f32[17,128,512]{2,1,0:T(8,128)} %subtract_divide_fusion.1, f32[16,128,512]{2,1,0:T(8,128)S(1)} %copy-done.10, f32[16,128,511]{2,1,0:T(8,128)} %slice.580, f32[22,134,512]{2,1,0:T(8,128)S(1)} %bitcast.84), kind=kLoop, calls=%fused_computation.162 | loop fusion | flops 9437184 | bytes 33546240 | tf_op jit(solution)/shard_map/sub | solution.py:124
  980.0 24.2 %fusion.77 = (f32[1,16,128,512]{3,2,1,0:T(8,128)}, f32[1,16,128,512]{3,2,1,0:T(8,128)}, f32[1,16,128,512]{3,2,1,0:T(8,128)}) fusion(f32[17,129,512]{2,1,0:T(8,128)} %fusion.10, f32[17,128,512]{2,1,0:T(8,128)} %copy-done.4, f32[17,128,1]{2,1,0:T(8,128)S(1)} %copy-done.12, f32[17,128,511]{2,1,0:T(8,128)} %get-tuple-element.56, ...), kind=kLoop, calls=%fused_computation.153 | loop fusion | flops 25165824 | bytes 71598080 | tf_op jit(solution)/shard_map/stack | solution.py:166
  1004.2 12.1 %pad_maximum_fusion.2 = f32[3,16,128,512]{3,2,1,0:T(8,128)} fusion(f32[1,16,128,512]{3,2,1,0:T(8,128)} %get-tuple-element.54, f32[1,16,128,512]{3,2,1,0:T(8,128)} %get-tuple-element.55, f32[1,16,128,512]{3,2,1,0:T(8,128)} %get-tuple-element.53), kind=kLoop, calls=%fused_computation.14 | loop fusion | flops 6291456 | bytes 25165824 | tf_op jit(solution)/shard_map/stack | solution.py:166
  (117 shorter events, 17.2 us)
Async XLA Ops:
  11.4 96.8 %all-to-all-start = ((f32[4,16,128,128]{3,1,0,2:T(8,128)}), f32[4,16,128,128]{3,1,0,2:T(8,128)}, u32[]{:S(2)}, u32[]{:S(2)}) async-start(f32[4,16,128,128]{3,1,0,2:T(8,128)} %copy.106), calls=%async_computation | async-start | bytes 8388608 | tf_op jit(solution)/shard_map/all_to_all | solution.py:205
  285.4 97.2 %all-to-all-start.1 = ((f32[16,1,65536]{2,1,0:T(1,128)}), f32[16,1,65536]{2,1,0:T(1,128)}, u32[]{:S(2)}, u32[]{:S(2)}) async-start(f32[16,1,65536]{2,1,0:T(1,128)} %reshape.119), calls=%async_computation.1 | async-start | bytes 8388608 | tf_op jit(solution)/shard_map/all_to_all | solution.py:227
  464.0 119.5 %collective-permute-start.1 = (f32[7,3,128,512]{3,2,1,0:T(8,128)}, f32[7,3,128,512]{3,2,1,0:T(8,128)}, u32[]{:S(2)}, u32[]{:S(2)}) collective-permute-start(f32[7,3,128,512]{3,2,1,0:T(8,128)} %copy.116), channel_id=1, source_target_pairs={{16,0},{17,1},{18,2},{19,3},{20,4},{21,5},{22,6},{23,7},{24,8},{25... | collective-permute-start | bytes 16515080 | tf_op jit(solution)/shard_map/ppermute | solution.py:26
  471.9 121.2 %collective-permute-start = (f32[7,3,128,512]{3,2,1,0:T(8,128)}, f32[7,3,128,512]{3,2,1,0:T(8,128)}, u32[]{:S(2)}, u32[]{:S(2)}) collective-permute-start(f32[7,3,128,512]{3,2,1,0:T(8,128)} %copy.114), channel_id=1, source_target_pairs={{0,16},{1,17},{2,18},{3,19},{4,20},{5,21},{6,22},{7,23},{8,24},{9,... | collective-permute-start | bytes 16515080 | tf_op jit(solution)/shard_map/ppermute | solution.py:25
  583.5 16.9 %slice-start.2 = ((s8[12582912]{0:T(1024)(128)(4,1)}), s8[4194304]{0:T(1024)(128)(4,1)S(1)}, s32[]{:S(2)}) async-start(s8[12582912]{0:T(1024)(128)(4,1)} %bitcast.85), calls=%async_computation.4 | async-start | bytes 8388608
  583.5 16.9 %slice-start.3 = ((s8[12582912]{0:T(1024)(128)(4,1)}), s8[4194304]{0:T(1024)(128)(4,1)S(1)}, s32[]{:S(2)}) async-start(s8[12582912]{0:T(1024)(128)(4,1)} %bitcast.85), calls=%async_computation.5 | async-start | bytes 8388608
  587.1 13.2 %copy-start.6 = (f32[7,3,128,512]{3,2,0,1:T(8,128)}, f32[7,3,128,512]{3,2,0,1:T(8,128)S(1)}, u32[]{:S(2)}) copy-start(f32[7,3,128,512]{3,2,0,1:T(8,128)S(1)} %copy_select_fusion) | copy-start | bytes 16515076
  593.0 7.3 slice-start.4
  593.0 7.3 copy-start.2
  593.1 8.8 copy-start.3
  605.0 27.8 %collective-permute-start.3 = (f32[7,22,3,512]{3,1,2,0:T(8,128)S(1)}, f32[7,22,3,512]{3,1,2,0:T(8,128)S(1)}, u32[]{:S(2)}, u32[]{:S(2)}) collective-permute-start(f32[7,22,3,512]{3,1,2,0:T(8,128)S(1)} %copy.119), channel_id=1, source_target_pairs={{1,0},{2,1},{3,2},{4,3},{5,4},{6,5},{7,6},{8,7},{9,8},{10,9},{11,1... | collective-permute-start | bytes 2838536 | tf_op jit(solution)/shard_map/ppermute | solution.py:26
  607.5 27.1 %collective-permute-start.2 = (f32[7,22,3,512]{3,1,2,0:T(8,128)S(1)}, f32[7,22,3,512]{3,1,2,0:T(8,128)S(1)}, u32[]{:S(2)}, u32[]{:S(2)}) collective-permute-start(f32[7,22,3,512]{3,1,2,0:T(8,128)S(1)} %copy.118), channel_id=1, source_target_pairs={{0,1},{1,2},{2,3},{3,4},{4,5},{5,6},{6,7},{7,8},{8,9},{9,10},{10,1... | collective-permute-start | bytes 2838536 | tf_op jit(solution)/shard_map/ppermute | solution.py:25
  727.2 7.8 copy-start
  727.2 20.3 %copy-start.1 = (f32[22,134,512]{2,1,0:T(8,128)}, f32[22,134,512]{2,1,0:T(8,128)S(1)}, u32[]{:S(2)}) copy-start(f32[22,134,512]{2,1,0:T(8,128)S(1)} %get-tuple-element.20) | copy-start | bytes 18112516
  742.2 10.5 %slice-start.19 = ((s8[6127616]{0:T(1024)(128)(4,1)}), s8[4194304]{0:T(1024)(128)(4,1)S(1)}, s32[]{:S(2)}) async-start(s8[6127616]{0:T(1024)(128)(4,1)} %bitcast.103), calls=%async_computation.21 | async-start | bytes 8388608
  747.4 5.3 slice-start.20
  829.4 6.8 copy-start.4
  829.4 6.8 slice-start.13
  831.2 5.0 slice-start.14
  836.3 11.2 %slice-start = ((s8[6127616]{0:T(1024)(128)(4,1)}), s8[4194304]{0:T(1024)(128)(4,1)S(1)}, s32[]{:S(2)}) async-start(s8[6127616]{0:T(1024)(128)(4,1)} %bitcast.83), calls=%async_computation.2 | async-start | bytes 8388608
  836.3 11.2 %slice-start.5 = ((s8[6127616]{0:T(1024)(128)(4,1)}), s8[4194304]{0:T(1024)(128)(4,1)S(1)}, s32[]{:S(2)}) async-start(s8[6127616]{0:T(1024)(128)(4,1)} %bitcast.87), calls=%async_computation.7 | async-start | bytes 8388608
  836.9 6.5 copy-start.5
  836.9 10.6 %slice-start.1 = ((s8[6127616]{0:T(1024)(128)(4,1)}), s8[1933312]{0:T(1024)(128)(4,1)S(1)}, s32[]{:S(2)}) async-start(s8[6127616]{0:T(1024)(128)(4,1)} %bitcast.83), calls=%async_computation.3 | async-start | bytes 3866624
  836.9 10.6 %slice-start.6 = ((s8[6127616]{0:T(1024)(128)(4,1)}), s8[1933312]{0:T(1024)(128)(4,1)S(1)}, s32[]{:S(2)}) async-start(s8[6127616]{0:T(1024)(128)(4,1)} %bitcast.87), calls=%async_computation.8 | async-start | bytes 3866624
  843.4 4.2 copy-start.7
  845.1 3.9 copy-start.9
  846.5 1.0 copy-start.11
  849.1 21.5 %copy-start.14 = (pred[512]{0:T(512)(128)(4,1)S(1)}, pred[512]{0:T(512)(128)(4,1)}, u32[]{:S(2)}) copy-start(pred[512]{0:T(512)(128)(4,1)} %iota_compare_fusion.3) | copy-start | bytes 1540
  865.8 4.8 copy-start.8
  891.6 15.0 %slice-start.7 = ((s8[4456448]{0:T(1024)(128)(4,1)}), s8[4194304]{0:T(1024)(128)(4,1)S(1)}, s32[]{:S(2)}) async-start(s8[4456448]{0:T(1024)(128)(4,1)} %bitcast.89), calls=%async_computation.9 | async-start | bytes 8388608
  891.6 15.0 %slice-start.9 = ((s8[4456448]{0:T(1024)(128)(4,1)}), s8[4194304]{0:T(1024)(128)(4,1)S(1)}, s32[]{:S(2)}) async-start(s8[4456448]{0:T(1024)(128)(4,1)} %bitcast.91), calls=%async_computation.11 | async-start | bytes 8388608
  897.1 9.5 slice-start.8
  897.1 9.5 slice-start.10
  906.6 11.6 %slice-start.17 = ((s8[5013504]{0:T(1024)(128)(4,1)}), s8[4194304]{0:T(1024)(128)(4,1)S(1)}, s32[]{:S(2)}) async-start(s8[5013504]{0:T(1024)(128)(4,1)} %bitcast.101), calls=%async_computation.19 | async-start | bytes 8388608
  906.7 11.6 %slice-start.18 = ((s8[5013504]{0:T(1024)(128)(4,1)}), s8[819200]{0:T(1024)(128)(4,1)S(1)}, s32[]{:S(2)}) async-start(s8[5013504]{0:T(1024)(128)(4,1)} %bitcast.101), calls=%async_computation.20 | async-start | bytes 1638400
  918.3 5.4 slice-start.15
  918.3 5.4 slice-start.16
  923.7 5.0 slice-start.21
  923.7 6.7 slice-start.23
  923.7 7.9 slice-start.25
  923.7 7.9 slice-start.22
  923.7 7.9 slice-start.24
  923.7 8.0 slice-start.26
  931.7 48.3 %slice-start.11 = ((s8[6127616]{0:T(1024)(128)(4,1)}), s8[4194304]{0:T(1024)(128)(4,1)S(1)}, s32[]{:S(2)}) async-start(s8[6127616]{0:T(1024)(128)(4,1)} %bitcast.93), calls=%async_computation.13 | async-start | bytes 8388608
  948.2 20.9 %copy-start.10 = (f32[16,128,512]{2,1,0:T(8,128)S(1)}, f32[16,128,512]{2,1,0:T(8,128)}, u32[]{:S(2)}) copy-start(f32[16,128,512]{2,1,0:T(8,128)} %divide_select_fusion) | copy-start | bytes 12582916
  948.2 31.8 %slice-start.12 = ((s8[6127616]{0:T(1024)(128)(4,1)}), s8[1933312]{0:T(1024)(128)(4,1)S(1)}, s32[]{:S(2)}) async-start(s8[6127616]{0:T(1024)(128)(4,1)} %bitcast.93), calls=%async_computation.14 | async-start | bytes 3866624
  969.2 10.8 %copy-start.12 = (f32[17,128,1]{2,1,0:T(8,128)S(1)}, f32[17,128,1]{2,1,0:T(8,128)}, u32[]{:S(2)}) copy-start(f32[17,128,1]{2,1,0:T(8,128)} %get-tuple-element.58) | copy-start | bytes 26116
  969.2 10.8 %copy-start.13 = (f32[16,129,1]{2,1,0:T(8,128)S(1)}, f32[16,129,1]{2,1,0:T(8,128)}, u32[]{:S(2)}) copy-start(f32[16,129,1]{2,1,0:T(8,128)} %get-tuple-element.61) | copy-start | bytes 24772
where the time goes:
time: 1020 us
  other arithmetic  409 us (40%)
  waiting for transfers between devices  232 us (23%)
  local copies, waits for them, and re-layouts  220 us (22%)
  matrix products  128 us (13%)
  starting transfers between devices  25 us (2%)
    ppermute x2, waiting for transfers between devices, extended(): after = lax.ppermute(leading, axis, down)  128 us
    dot_general x1, matrix products, per_device(): lax.dot_general(spectrum.reshape(-1, NP), fourier_basis, (((1,), (1,)), (...  94.4 us
    all_to_all x1, waiting for transfers between devices, per_device(): lax.all_to_all(smoothed, 'phi', split_axis=3, concat_axis=2, tiled=True)  78.6 us
    dot_general x1, other arithmetic, per_device(): jnp.dot(lines.reshape(-1, NP), fourier_basis, precision=lax.Precision.HIG...  67.5 us
    concatenate x1, other arithmetic, extended(): value = jnp.concatenate([before, value, after], axis=dim)  57.4 us
    unnamed x86, local copies, waits for them, and re-layouts  55.7 us
    sub x2, other arithmetic, edge_values(): to_right = right_face - centre  39.5 us
    div x2, other arithmetic, hll_flux(): (upwind + slowest * fastest * (dens_right - dens_left)) / (fastest - slow...  37.5 us
  transfers between devices with their start and end apart: 6, of which 5 were waited for; matrix products, arithmetic and copies ran while one was open for 9% of the time, Pallas kernels for 0%

commit v1 on v0

v1 whole, which is shorter than its diff:
```python
import math

import jax
import jax.numpy as jnp
import numpy as np
from jax import lax
from jax.experimental import pallas as pl
from jax.experimental.pallas import tpu as pltpu
from jax.sharding import PartitionSpec as P

NPOL = 128
RADIX = 16
FRONT = 16
TILE = 8

COURANT_RAD = 0.3
COURANT_POL = 0.25
COURANT_AZI = 0.35
SOUND_SPEED = 1.0


def rotate(value, angle):
    re, im = value
    c, s = math.cos(angle), math.sin(angle)
    if im is None:
        return (re * c, re * s)
    return (re * c - im * s, re * s + im * c)


def add(a, b, sign=1.0):
    def part(x, y):
        if y is None:
            return x
        if x is None:
            return y if sign > 0 else -y
        return x + y if sign > 0 else x - y

    return (part(a[0], b[0]), part(a[1], b[1]))


def conj(a):
    return (a[0], None if a[1] is None else -a[1])


def real_fft(xs):
    n = len(xs)
    if n == 1:
        return [(xs[0], None)]
    if n == 2:
        return [(xs[0] + xs[1], None), (xs[0] - xs[1], None)]
    even, odd = real_fft(xs[0::2]), real_fft(xs[1::2])
    half = n // 2

    def at(spec, k):
        return spec[k] if k <= half // 2 else conj(spec[half - k])

    result = []
    for k in range(half + 1):
        e, o = at(even, k % half), at(odd, k % half)
        if k == 0:
            result.append(add(e, o))
        elif k == half:
            result.append(add(e, o, -1.0))
        elif 4 * k == n:
            result.append((e[0], -o[0]))
        else:
            result.append(add(e, rotate(o, -2.0 * math.pi * k / n)))
    return result


def real_ifft(spec, n):
    if n == 2:
        a, b = spec[0][0], spec[1][0]
        return [a + b, a - b]
    half = n // 2
    even, odd = [], []
    for k in range(half // 2 + 1):
        a, b = spec[k], conj(spec[half - k])
        if k == 0:
            a, b = (spec[0][0], None), (spec[half][0], None)
            even.append(add(a, b))
            odd.append(add(a, b, -1.0))
        elif 4 * k == n:
            even.append((2.0 * spec[k][0], None))
            odd.append((-2.0 * spec[k][1], None))
        else:
            even.append(add(a, b))
            odd.append(rotate(add(a, b, -1.0), 2.0 * math.pi * k / n))
    evens, odds = real_ifft(even, half), real_ifft(odd, half)
    return [v for pair in zip(evens, odds) for v in pair]


def filter_tables(cells, theta_count):
    inner = cells // RADIX
    half_polar = NPOL // 2
    k2 = np.arange(RADIX // 2 + 1)[:, None]
    mode = k2 + RADIX * np.arange(inner)[None, :]
    angle = 2.0 * np.pi / cells * ((mode[:, :, None] * np.arange(inner)) % cells)
    cos, sin = np.cos(angle), np.sin(angle)
    forward = np.concatenate(
        [np.concatenate([cos, sin], 2), np.concatenate([-sin, cos], 2)], 1
    ).astype(np.float32)
    rows = np.arange(NPOL)
    theta = np.where(rows < half_polar, rows, theta_count - NPOL + rows)
    row_square = np.sin(np.pi * (theta + 0.5) / theta_count) ** 2
    edge = np.sin(np.pi * (half_polar + 0.5) / theta_count)
    mode_square = (edge * np.sin(np.pi * mode / cells)) ** 2
    damping = row_square / np.maximum(row_square, mode_square[:, :, None])
    return forward, (damping / cells).astype(np.float32)


def filter_kernel(group, inner, blocks, x_ref, basis_ref, damp_ref, out_ref):
    azimuth = x_ref.shape[2]

    def slab(d):
        parts = [
            x_ref[d * blocks : (d + 1) * blocks, g].reshape(inner, NPOL) for g in range(group)
        ]
        return jnp.concatenate(parts, axis=1) if group > 1 else parts[0]

    spectrum = real_fft([slab(d) for d in range(RADIX)])
    filtered = []
    for k, (re, im) in enumerate(spectrum):
        basis = basis_ref[k]
        if im is None:
            forward = basis[:, :inner]
            stacked = re
        else:
            forward = basis
            stacked = jnp.concatenate([re, im], axis=0)
        modes = jnp.dot(
            forward, stacked, precision=lax.Precision.HIGHEST, preferred_element_type=jnp.float32
        )
        damp = damp_ref[k]
        damp = jnp.concatenate([damp, damp], axis=0)
        if group > 1:
            damp = jnp.concatenate([damp] * group, axis=1)
        back = lax.dot_general(
            forward,
            modes * damp,
            (((0,), (0,)), ((), ())),
            precision=lax.Precision.HIGHEST,
            preferred_element_type=jnp.float32,
        )
        filtered.append((back, None) if im is None else (back[:inner], back[inner:]))
    for d, value in enumerate(real_ifft(filtered, RADIX)):
        for g in range(group):
            out_ref[d * blocks : (d + 1) * blocks, g] = value[
                :, g * NPOL : (g + 1) * NPOL
            ].reshape(blocks, azimuth, NPOL)


def filter_lines(lines, theta_count):
    devices, pairs, azimuth, _ = lines.shape
    cells = devices * azimuth
    inner = cells // RADIX
    blocks = inner // azimuth
    group = 2 if pairs % 2 == 0 else 1
    forward, damping = filter_tables(cells, theta_count)
    spec = pl.BlockSpec((devices, group, azimuth, NPOL), lambda p: (0, p, 0, 0))
    return pl.pallas_call(
        lambda *refs: filter_kernel(group, inner, blocks, *refs),
        grid=(pairs // group,),
        in_specs=[
            spec,
            pl.BlockSpec(forward.shape, lambda p: (0, 0, 0)),
            pl.BlockSpec(damping.shape, lambda p: (0, 0, 0)),
        ],
        out_specs=spec,
        out_shape=jax.ShapeDtypeStruct(lines.shape, jnp.float32),
        compiler_params=pltpu.CompilerParams(vmem_limit_bytes=56 * 1024 * 1024),
        name="polar_filter",
    )(lines, jnp.asarray(forward), jnp.asarray(damping))


def interface_value(outer_left, inner_left, inner_right, outer_right):
    guess = 7.0 / 12.0 * (inner_left + inner_right) - 1.0 / 12.0 * (outer_left + outer_right)
    low = jnp.minimum(inner_left, inner_right)
    return jnp.minimum(jnp.maximum(guess, low), jnp.maximum(inner_left, inner_right))


def limited(centre, left_face, right_face):
    to_left = left_face - centre
    to_right = right_face - centre
    reach_right = 2.0 * jnp.abs(to_right)
    reach_left = 2.0 * jnp.abs(to_left)
    left = jnp.minimum(jnp.maximum(to_left, -reach_right), reach_right)
    right = jnp.minimum(jnp.maximum(to_right, -reach_left), reach_left)
    return centre + left, centre + right


def edges(q):
    left_face = interface_value(q[0], q[1], q[2], q[3])
    right_face = interface_value(q[1], q[2], q[3], q[4])
    return limited(q[2], left_face, right_face)


def hll_flux(dens_left, dens_right, speed_left, speed_right):
    slowest = jnp.minimum(jnp.minimum(speed_left, speed_right) - SOUND_SPEED, 0.0)
    fastest = jnp.maximum(jnp.maximum(speed_left, speed_right) + SOUND_SPEED, 0.0)
    upwind = fastest * dens_left * speed_left - slowest * dens_right * speed_right
    return (upwind + slowest * fastest * (dens_right - dens_left)) / (fastest - slowest)


PRIM_ROWS = ((0, 0, 3), (3, 3, 3), (1, 6, 1), (2, 7, 1))
MAG_ROWS_LOW = ((4, 8, 1), (5, 9, 1), (6, 10, 1))
MAG_ROWS_HIGH = ((4, 8, 1), (5, 9, 1), (6, 10, 2))
PACKED = 16


def stencil_kernel(
    radial, azimuth, dens, vel, mag, polar, g2, g2p, g5, g5p, gbr, side, sidep,
    dens_out, mag_out,
    s0, s1, s2, s3, s4, s5, s6, er, et, ep, carry_rho, carry_u, carry_flux,
):
    state = (s0, s1, s2, s3, s4, s5, s6)
    t = pl.program_id(0)
    layer = t - 3
    width = dens.shape[-1]
    half = NPOL // 2
    slot = lax.rem(t, 8)
    own = slice(FRONT, FRONT + azimuth)

    def merge(raw, pol):
        lane = lax.broadcasted_iota(jnp.int32, pol.shape, 1)
        return jnp.concatenate(
            [
                jnp.where(lane < half, pol, raw[:, :NPOL]),
                raw[:, NPOL : width - NPOL],
                jnp.where(lane >= half, pol, raw[:, width - NPOL :]),
            ],
            axis=1,
        )

    @pl.when((layer >= 0) & (layer < radial))
    def _():
        s0[slot, own] = merge(dens[0], polar[0, 0])
        for c in range(3):
            state[1 + c][slot, own] = merge(vel[c, 0], polar[1 + c, 0])
            state[4 + c][slot, own] = mag[c, 0]

    @pl.when((layer < 0) | (layer >= radial))
    def _():
        s0[slot, own] = merge(g2[0, 0], g2p[0, 0])
        s1[slot, own] = merge(g2[0, 1], g2p[0, 1])

    @pl.when((layer == -1) | (layer == radial))
    def _():
        s2[slot, own] = merge(g5[0, 0], g5p[0, 0])
        s3[slot, own] = merge(g5[0, 1], g5p[0, 1])
        for c in range(3):
            state[4 + c][slot, own] = g5[0, 2 + c]

    @pl.when(layer == radial + 1)
    def _():
        s4[slot, own] = gbr[...]

    @pl.when((layer >= -1) & (layer <= radial + 1))
    def _():
        low = merge(side[0, 0, :8], sidep[0, 0])
        high = merge(side[1, 0, :8], sidep[1, 0])
        for f, row, count in PRIM_ROWS:
            state[f][slot, FRONT - count : FRONT] = low[row : row + count]
            state[f][slot, FRONT + azimuth : FRONT + azimuth + count] = high[row : row + count]
        for f, row, count in MAG_ROWS_LOW:
            state[f][slot, FRONT - count : FRONT] = side[0, 0, row : row + count]
        for f, row, count in MAG_ROWS_HIGH:
            state[f][slot, FRONT + azimuth : FRONT + azimuth + count] = side[
                1, 0, row : row + count
            ]

    shape = (TILE, width)
    lane = lax.broadcasted_iota(jnp.int32, shape, 1)
    sub = lax.broadcasted_iota(jnp.int32, shape, 0)

    def shifted(ref, index, base, off):
        here = ref[index, pl.ds(base, TILE), :]
        if off > 0:
            other = ref[index, pl.ds(base + TILE, TILE), :]
            return pltpu.roll(jnp.where(sub < off, other, here), TILE - off, 0)
        if off < 0:
            other = ref[index, pl.ds(base - TILE, TILE), :]
            return pltpu.roll(jnp.where(sub >= TILE + off, other, here), -off, 0)
        return here

    def at(ref, d, base, off=0):
        return shifted(ref, lax.rem(t - 3 + d + 8, 8), base, off)

    def up(x):
        return jnp.where(lane == width - 1, x, pltpu.roll(x, width - 1, 1))

    def down(x):
        return jnp.where(lane == 0, x, pltpu.roll(x, 1, 1))

    def before(x, previous):
        return jnp.where(sub == 0, pltpu.roll(previous, 1, 0), pltpu.roll(x, 1, 0))

    def azimuth_step(base, right_rho, right_u):
        left_r, next_r = edges([at(s0, 0, base, o) for o in (-1, 0, 1, 2, 3)])
        left_u, next_u = edges([at(s3, 0, base, o) for o in (-1, 0, 1, 2, 3)])
        flux = hll_flux(before(next_r, right_rho), left_r, before(next_u, right_u), left_u)
        return next_r, next_u, flux

    def theta_edges(q):
        below = down(q)
        face = interface_value(down(below), below, q, up(q))
        above = jnp.where(lane == width - 1, q, pltpu.roll(face, width - 1, 1))
        return limited(q, face, above)

    here = lax.rem(t, 4)

    def emf_tile(j, _):
        base = pl.multiple_of(FRONT - TILE + j * TILE, TILE)
        u_r, u_t, u_p = (at(s, 1, base) for s in (s1, s2, s3))
        b_r = 0.5 * (at(s4, 1, base) + at(s4, 2, base))
        b_t = at(s5, 1, base)
        b_t = 0.5 * (b_t + up(b_t))
        b_p = 0.5 * (at(s6, 1, base) + at(s6, 1, base, 1))
        rows = pl.ds(base, TILE)
        er[here, rows, :] = u_p * b_t - u_t * b_p
        et[here, rows, :] = u_r * b_p - u_p * b_r
        ep[here, rows, :] = u_t * b_r - u_r * b_t
        return 0

    @pl.when(t >= 4)
    def _():
        lax.fori_loop(0, azimuth // TILE + 2, emf_tile, 0)

    def emf(ref, d, base, off=0):
        return shifted(ref, lax.rem(t - 1 + d + 4, 4), base, off)

    def tile(j, carry):
        right_rho, right_u, flux_low = carry
        start = pl.multiple_of(j * TILE, TILE)
        base = pl.multiple_of(FRONT + j * TILE, TILE)
        rows = pl.ds(start, TILE)

        left_r, right_r = edges([at(s0, d, base) for d in (-1, 0, 1, 2, 3)])
        left_u, right_v = edges([at(s1, d, base) for d in (-1, 0, 1, 2, 3)])
        flux = hll_flux(carry_rho[rows, :], left_r, carry_u[rows, :], left_u)
        total = COURANT_RAD * (flux - carry_flux[rows, :])
        carry_rho[rows, :] = right_r
        carry_u[rows, :] = right_v
        carry_flux[rows, :] = flux

        right_rho, right_u, flux = azimuth_step(base, right_rho, right_u)
        total = total + COURANT_AZI * (flux - before(flux, flux_low))
        flux_low = flux

        rho = at(s0, 0, base)
        left_r, right_r = theta_edges(rho)
        left_u, right_v = theta_edges(at(s2, 0, base))
        theta_flux = hll_flux(down(right_r), left_r, down(right_v), left_u)
        theta_flux = jnp.where(lane == 0, 0.0, theta_flux)
        above = jnp.where(lane == width - 1, 0.0, pltpu.roll(theta_flux, width - 1, 1))
        total = total + COURANT_POL * (above - theta_flux)
        dens_out[0, rows, :] = rho - total

        er_low, er_here, er_high = (emf(er, 0, base, o) for o in (-1, 0, 1))
        ep_low, ep_here, ep_high = (emf(ep, d, base) for d in (-1, 0, 1))
        below_k = emf(et, -1, base, -1)
        edge_a = 0.5 * (ep_low + ep_here)
        edge_r = 0.5 * (er_low + er_here)
        mixed = (0.5 * COURANT_RAD) * (ep_high - ep_low) - (0.5 * COURANT_AZI) * (er_high - er_low)
        across = emf(et, -1, base, 1) + emf(et, 0, base, 1) - below_k - emf(et, 0, base, -1)
        along = emf(et, 1, base, -1) + emf(et, 1, base) - below_k - emf(et, -1, base)
        mag_out[0, 0, rows, :] = (
            at(s4, 0, base)
            - (0.5 * COURANT_POL) * (up(edge_a) - down(edge_a))
            + (0.25 * COURANT_AZI) * across
        )
        mag_out[1, 0, rows, :] = at(s5, 0, base) + 0.5 * (down(mixed) + mixed)
        mag_out[2, 0, rows, :] = (
            at(s6, 0, base)
            - (0.25 * COURANT_RAD) * along
            + (0.5 * COURANT_POL) * (up(edge_r) - down(edge_r))
        )
        return right_rho, right_u, flux_low

    @pl.when(t >= 4)
    def _():
        zero = jnp.zeros(shape, jnp.float32)
        first = azimuth_step(FRONT - TILE, zero, zero)
        lax.fori_loop(0, azimuth // TILE, tile, first)


def stencil(density, velocity, magnetic, polar, ghosts):
    radial, azimuth, width = density.shape
    g2, g2p, g5, g5p, gbr, side, sidep = ghosts

    def own(t):
        return jnp.clip(t - 3, 0, radial - 1)

    def outer(t):
        return jnp.where(t < 3, t, jnp.clip(t - radial, 2, 5))

    def near(t):
        return jnp.where(t < radial + 3, 0, 1)

    def flank(t):
        return jnp.clip(t - 2, 0, radial + 2)

    def out(t):
        return jnp.clip(t - 6, 0, radial - 1)

    rows = FRONT + azimuth + 2 * TILE
    scratch = (
        [pltpu.VMEM((8, rows, width), jnp.float32)] * 7
        + [pltpu.VMEM((4, rows, width), jnp.float32)] * 3
        + [pltpu.VMEM((azimuth, width), jnp.float32)] * 3
    )
    return pl.pallas_call(
        lambda *refs: stencil_kernel(radial, azimuth, *refs),
        grid=(radial + 6,),
        in_specs=[
            pl.BlockSpec((1, azimuth, width), lambda t: (own(t), 0, 0)),
            pl.BlockSpec((3, 1, azimuth, width), lambda t: (0, own(t), 0, 0)),
            pl.BlockSpec((3, 1, azimuth, width), lambda t: (0, own(t), 0, 0)),
            pl.BlockSpec((4, 1, azimuth, NPOL), lambda t: (0, own(t), 0, 0)),
            pl.BlockSpec((1, 2, azimuth, width), lambda t: (outer(t), 0, 0, 0)),
            pl.BlockSpec((1, 2, azimuth, NPOL), lambda t: (outer(t), 0, 0, 0)),
            pl.BlockSpec((1, 5, azimuth, width), lambda t: (near(t), 0, 0, 0)),
            pl.BlockSpec((1, 2, azimuth, NPOL), lambda t: (near(t), 0, 0, 0)),
            pl.BlockSpec((azimuth, width), lambda t: (0, 0)),
            pl.BlockSpec((2, 1, PACKED, width), lambda t: (0, flank(t), 0, 0)),
            pl.BlockSpec((2, 1, 8, NPOL), lambda t: (0, flank(t), 0, 0)),
        ],
        out_specs=[
            pl.BlockSpec((1, azimuth, width), lambda t: (out(t), 0, 0)),
            pl.BlockSpec((3, 1, azimuth, width), lambda t: (0, out(t), 0, 0)),
        ],
        out_shape=[
            jax.ShapeDtypeStruct(density.shape, jnp.float32),
            jax.ShapeDtypeStruct(magnetic.shape, jnp.float32),
        ],
        scratch_shapes=scratch,
        compiler_params=pltpu.CompilerParams(
            dimension_semantics=("arbitrary",), vmem_limit_bytes=62 * 1024 * 1024
        ),
        name="section",
    )(density, velocity, magnetic, polar, g2, g2p, g5, g5p, gbr, side, sidep)


def chain(devices, wrap):
    up = [(i, (i + 1) % devices) for i in range(devices if wrap else devices - 1)]
    return up, [(j, i) for i, j in up]


def radial_ghosts(prim, mag):
    rho, u_r, u_t, u_p = prim
    radial = rho.shape[0]

    def sides(low, high):
        devices = lax.axis_size("row")
        up, down = chain(devices, False)
        return lax.ppermute(high, "row", up), lax.ppermute(low, "row", down)

    low = [rho[:3], u_r[:3], u_t[:1], u_p[:1]]
    high = [rho[-3:], u_r[-3:], u_t[-1:], u_p[-1:]]
    if mag is not None:
        low += [mag[0][:2], mag[1][:1], mag[2][:1]]
        high += [mag[0][-1:], mag[1][-1:], mag[2][-1:]]
    below, above = sides(jnp.concatenate(low, 0), jnp.concatenate(high, 0))
    first = lax.axis_index("row") == 0
    last = lax.axis_index("row") == lax.axis_size("row") - 1

    below = jnp.where(first, jnp.concatenate(repeated(high, prim, mag, 0), 0), below)
    above = jnp.where(last, jnp.concatenate(repeated(low, prim, mag, radial - 1), 0), above)
    outer = jnp.stack(
        [jnp.stack([below[i], below[3 + i]]) for i in range(3)]
        + [jnp.stack([above[i], above[3 + i]]) for i in range(3)]
    )
    if mag is None:
        near = jnp.stack([below[6:8], above[6:8]])
        return outer, near, None
    near = jnp.stack([below[6:11], jnp.concatenate([above[6:9], above[10:12]])])
    return outer, near, above[9]


def repeated(parts, prim, mag, layer):
    fields = list(prim) + ([] if mag is None else list(mag))
    return [jnp.broadcast_to(f[layer], p.shape) for f, p in zip(fields, parts)]


def azimuth_ghosts(prim, mag, outer, near, beyond):
    def rows(sl):
        groups = [
            (prim[0], outer[2, 0], outer[3, 0], 3),
            (prim[3], near[0, 1], near[1, 1], 3),
            (prim[1], outer[2, 1], outer[3, 1], 1),
            (prim[2], near[0, 0], near[1, 0], 1),
        ]
        if mag is not None:
            groups += [(mag[c], near[0, 2 + c], near[1, 2 + c], 1 if c < 2 else 2) for c in range(3)]
        parts = []
        for n, (field, below, above, count) in enumerate(groups):
            pick = sl(count)
            extra = beyond if (beyond is not None and n == 4) else above
            parts.append(
                jnp.concatenate(
                    [below[None, pick], field[:, pick], above[None, pick], extra[None, pick]], 0
                )
            )
        packed = jnp.concatenate(parts, 1)
        size = 8 if mag is None else PACKED
        return jnp.pad(packed, ((0, 0), (0, size - packed.shape[1]), (0, 0)))

    azimuth = prim[0].shape[1]
    up, down = chain(lax.axis_size("phi"), True)
    high = rows(lambda n: slice(azimuth - (1 if n == 2 else n), azimuth))
    low = rows(lambda n: slice(0, n))
    return jnp.stack([lax.ppermute(high, "phi", up), lax.ppermute(low, "phi", down)])


def per_device(density, velocity, magnetic):
    radial, azimuth, width = density.shape
    half = NPOL // 2
    devices = lax.axis_size("phi")
    prim = [density, velocity[0], velocity[1], velocity[2]]
    mag = [magnetic[0], magnetic[1], magnetic[2]]
    rows = jnp.stack(
        [jnp.concatenate([p[..., :half], p[..., width - half :]], axis=-1) for p in prim]
    )
    lines = rows.reshape(devices, -1, azimuth, NPOL)
    lines = lax.all_to_all(lines, "phi", split_axis=0, concat_axis=0, tiled=True)
    lines = filter_lines(lines, width)
    lines = lax.all_to_all(lines, "phi", split_axis=0, concat_axis=0, tiled=True)
    polar = lines.reshape(4, radial, azimuth, NPOL)

    g2, g5, gbr = radial_ghosts(prim, mag)
    side = azimuth_ghosts(prim, mag, g2, g5, gbr)
    smooth = [polar[c] for c in range(4)]
    g2p, g5p, _ = radial_ghosts(smooth, None)
    sidep = azimuth_ghosts(smooth, None, g2p, g5p, None)
    return tuple(
        stencil(density, velocity, magnetic, polar, (g2, g2p, g5, g5p, gbr, side, sidep))
    )


def solution(mesh):
    placed = (P("row", "phi", None), P(None, "row", "phi", None), P(None, "row", "phi", None))
    return jax.shard_map(
        per_device,
        mesh=mesh,
        in_specs=placed,
        out_specs=(P("row", "phi", None), P(None, "row", "phi", None)),
        check_vma=False,
    )
```

time: 1020 us -> 436 us (0.43)
  other arithmetic: 409 us -> 33 us
  Pallas kernels: 0 us -> 168 us
  local copies, waits for them, and re-layouts: 220 us -> 79 us
  matrix products: 128 us -> 0 us
  waiting for transfers between devices: 232 us -> 117 us
    pallas_call x0 -> x2, Pallas kernels: none -> 168 us  [the longest x1 154 us: stencil(): pl.pallas_call(lambda *refs: stencil_kernel(radial, azimuth, *refs), grid...]
    dot_general x2 -> x0, matrix products: 128 us -> none  [the longest x1 94.4 us: per_device(): lax.dot_general(spectrum.reshape(-1, NP), fourier_basis, (((1,), (1,)), (...]
    ppermute x4 -> x8, waiting for transfers between devices: 133 us -> 35 us  [the longest x4 22.6 us: sides(): return (lax.ppermute(high, 'row', up), lax.ppermute(low, 'row', down))]
    dot_general x2 -> x0, other arithmetic: 67.8 us -> none  [the longest x1 67.5 us: per_device(): jnp.dot(lines.reshape(-1, NP), fourier_basis, precision=lax.Precision.HIG...]
    slice x23 -> x25, local copies, waits for them, and re-layouts: 80.8 us -> 20.3 us  [the longest x11 12.3 us: rows(): field[:, pick]]
    concatenate x2 -> x17, other arithmetic: 69 us -> 13.9 us  [the longest x14 13.8 us: rows(): jnp.concatenate([below[None, pick], field[:, pick], above[None, pick], ex...]
    sub x4 -> x0, other arithmetic: 50.3 us -> none  [the longest x2 39.5 us: edge_values(): to_right = right_face - centre]
    neg x2 -> x0, other arithmetic: 39 us -> none  [the longest x1 23.7 us: advance(): azimuth_emf = -(speed_r * polar_cell - speed_t * radial_cell)]
  transfers between devices with their start and end apart: 6 -> 10, of which waited for: 5 -> 8; matrix products, arithmetic and copies ran while one was open for 9% -> 19% of each run, Pallas kernels for 0% -> 3%
where the time goes in v1:
time: 436 us; the launch traced here: 434 us
  Pallas kernels  168 us (39%)
  waiting for transfers between devices  117 us (27%)
  local copies, waits for them, and re-layouts  79 us (18%)
  starting transfers between devices  35.1 us (8%)
  other arithmetic  33 us (8%)
    pallas_call x1, Pallas kernels, stencil(): pl.pallas_call(lambda *refs: stencil_kernel(radial, azimuth, *refs), grid...  154 us
    all_to_all x2, waiting for transfers between devices, per_device(): lax.all_to_all(lines, 'phi', split_axis=0, concat_axis=0, tiled=True)  82.4 us
    ppermute x4, waiting for transfers between devices, sides(): return (lax.ppermute(high, 'row', up), lax.ppermute(low, 'row', down))  22.6 us
    unnamed x42, local copies, waits for them, and re-layouts  21.3 us
    pallas_call x1, Pallas kernels, filter_lines(): pl.pallas_call(lambda *refs: filter_kernel(group, inner, blocks, *refs),...  14.5 us
    concatenate x14, other arithmetic, rows(): jnp.concatenate([below[None, pick], field[:, pick], above[None, pick], ex...  13.8 us
    all_to_all x2, starting transfers between devices, per_device(): lax.all_to_all(lines, 'phi', split_axis=0, concat_axis=0, tiled=True)  13.6 us
    slice x11, local copies, waits for them, and re-layouts, rows(): field[:, pick]  12.3 us
  transfers between devices with their start and end apart: 10, of which 8 were waited for; matrix products, arithmetic and copies ran while one was open for 19% of the time, Pallas kernels for 3%

profile of v1, /device:TPU:13, one launch (start us, length us, event | category | flops | bytes accessed | tf_op | source)
XLA Modules:
  0.0 433.9 jit_solution(10420205831258371255)
XLA Ops:
  0.6 1.9 fusion.17
  2.5 10.3 %slice_bitcast_fusion.5 = (f32[16,128,512]{2,1,0:T(8,128)}, f32[16,128,512]{2,1,0:T(8,128)S(1)}, f32[16,128,512]{2,1,0:T(8,128)}) fusion(f32[3,16,128,512]{3,2,1,0:T(8,128)} %refs_1_.2), kind=kLoop, calls=%fused_computation.6 | loop fusion | bytes 25165824 | tf_op jit(solution)/shard_map/squeeze | solution.py:519
  13.2 3.3 copy-done.1
  16.5 2.3 fusion.18
  20.2 2.3 pad_maximum_fusion
  22.5 6.5 %all-to-all-start = ((f32[16,4,128,128]{3,2,1,0:T(8,128)}), f32[16,4,128,128]{3,2,1,0:T(8,128)}, u32[]{:S(2)}, u32[]{:S(2)}) async-start(f32[16,4,128,128]{3,2,1,0:T(8,128)} %bitcast.228), calls=%async_computation | async-start | bytes 8388608 | tf_op jit(solution)/shard_map/all_to_all | solution.py:525
  29.0 1.0 slice_bitcast_fusion.12
  30.0 1.1 slice_bitcast_fusion.9
  31.1 1.1 slice_bitcast_fusion.8
  32.6 2.8 slice_dynamic-update-slice_fusion
  35.3 2.7 bitcast_dynamic-update-slice_fusion
  38.0 1.9 bitcast_dynamic-update-slice_fusion.19
  40.0 2.1 bitcast_dynamic-update-slice_fusion.17
  42.0 1.0 bitcast_dynamic-update-slice_fusion.8
  43.0 1.8 bitcast_dynamic-update-slice_fusion.7
  44.8 1.9 bitcast_dynamic-update-slice_fusion.2
  46.7 1.9 bitcast_dynamic-update-slice_fusion.14
  48.6 2.0 bitcast_dynamic-update-slice_fusion.12
  50.7 1.6 copy-done.4
  52.2 1.3 collective-permute-start
  53.5 7.3 %collective-permute-start.1 = (f32[12,128,512]{2,1,0:T(8,128)}, f32[12,128,512]{2,1,0:T(8,128)}, u32[]{:S(2)}, u32[]{:S(2)}) collective-permute-start(f32[12,128,512]{2,1,0:T(8,128)} %get-tuple-element.5), channel_id=1, source_target_pairs={{16,0},{17,1},{18,2},{19,3},{20,4},{21,5},{22,6},{23,7},{24,8},{25... | collective-permute-start | bytes 9437192 | tf_op jit(solution)/shard_map/ppermute | solution.py:456
  60.8 10.0 %slice_bitcast_fusion = (f32[16,128,512]{2,1,0:T(8,128)}, f32[16,128,512]{2,1,0:T(8,128)}, f32[16,128,512]{2,1,0:T(8,128)}) fusion(f32[3,16,128,512]{3,2,1,0:T(8,128)} %refs_2_.2), kind=kLoop, calls=%fused_computation.1 | loop fusion | bytes 25165824 | tf_op jit(solution)/shard_map/squeeze | solution.py:520
  70.8 1.6 slice.901
  72.4 1.0 slice.922
  73.4 1.7 fusion.10
  75.1 1.8 fusion.15
  76.9 1.8 fusion.14
  78.7 40.6 %all-to-all-done.refs_0_ = f32[16,4,128,128]{3,2,1,0:T(8,128)} async-done(((f32[16,4,128,128]{3,2,1,0:T(8,128)}), f32[16,4,128,128]{3,2,1,0:T(8,128)}, u32[]{:S(2)}, u32[]{:S(2)}) %all-to-all-start) | async-done | bytes 4194336 | tf_op jit(solution)/shard_map/all_to_all | solution.py:525
  119.3 14.5 %polar_filter.1 = f32[16,4,128,128]{3,2,1,0:T(8,128)} custom-call(f32[16,4,128,128]{3,2,1,0:T(8,128)} %all-to-all-done.refs_0_, f32[9,256,256]{2,1,0:T(8,128)} %constant.16.clone.refs_1_, f32[9,128,128]{2,1,0:T(8,128)} %constant.17.clone.refs_2_), custom_call_target="tpu_custom_call" | custom-call | tf_op jit(solution)/shard_map/polar_filter/pallas_call | solution.py:161
  133.7 7.0 %all-to-all-start.1 = ((f32[16,4,128,128]{3,2,1,0:T(8,128)}), f32[16,4,128,128]{3,2,1,0:T(8,128)}, u32[]{:S(2)}, u32[]{:S(2)}) async-start(f32[16,4,128,128]{3,2,1,0:T(8,128)} %polar_filter.1), calls=%async_computation.1 | async-start | bytes 8388608 | tf_op jit(solution)/shard_map/all_to_all | solution.py:527
  140.8 1.7 fusion.11
  142.4 1.0 bitcast_dynamic-update-slice_fusion.3
  143.4 2.7 fusion.12
  146.1 2.7 broadcast_select_fusion.1
  149.2 0.9 fusion.2
  150.1 0.8 fusion.3
  154.6 1.1 slice_bitcast_fusion.7
  162.2 2.2 concatenate.145
  164.4 0.9 pad.9
  166.1 1.4 pad_maximum_fusion.18
  167.5 1.4 pad_maximum_fusion.21
  168.9 1.4 pad_maximum_fusion.22
  170.3 1.4 pad_maximum_fusion.20
  171.7 1.6 pad_maximum_fusion.12
  173.4 1.6 pad_maximum_fusion.13
  175.0 2.2 concatenate.137
  177.3 1.5 collective-permute-start.4
  178.8 1.9 constant_dynamic-update-slice_fusion.1
  180.6 1.8 constant_dynamic-update-slice_fusion
  183.3 0.9 fusion.5.refs_4_
  184.1 1.9 pad_maximum_fusion.1.refs_6_
  186.0 5.6 %collective-permute-done.4 = f32[19,16,512]{2,1,0:T(8,128)S(1)} collective-permute-done((f32[19,16,512]{2,1,0:T(8,128)S(1)}, f32[19,16,512]{2,1,0:T(8,128)S(1)}, u32[]{:S(2)}, u32[]{:S(2)}) %collective-permute-start.4) | collective-permute-done | bytes 622624 | tf_op jit(solution)/shard_map/ppermute | solution.py:512
  191.6 3.1 collective-permute-done.5
  194.7 1.1 pad_maximum_fusion.2.refs_9_
  195.8 41.8 %all-to-all-done.1 = f32[16,4,128,128]{3,2,1,0:T(8,128)} async-done(((f32[16,4,128,128]{3,2,1,0:T(8,128)}), f32[16,4,128,128]{3,2,1,0:T(8,128)}, u32[]{:S(2)}, u32[]{:S(2)}) %all-to-all-start.1) | async-done | bytes 4194336 | tf_op jit(solution)/shard_map/all_to_all | solution.py:527
  237.6 2.4 fusion.16
  240.3 2.2 collective-permute-start.3
  242.5 10.2 %collective-permute-done.3 = f32[8,128,128]{2,1,0:T(8,128)S(1)} collective-permute-done((f32[8,128,128]{2,1,0:T(8,128)S(1)}, f32[8,128,128]{2,1,0:T(8,128)S(1)}, u32[]{:S(2)}, u32[]{:S(2)}) %collective-permute-start.3) | collective-permute-done | bytes 524320 | tf_op jit(solution)/shard_map/ppermute | solution.py:456
  253.0 1.3 collective-permute-start.2
  254.3 12.4 %collective-permute-done.2 = f32[8,128,128]{2,1,0:T(8,128)S(1)} collective-permute-done((f32[8,128,128]{2,1,0:T(8,128)S(1)}, f32[8,128,128]{2,1,0:T(8,128)S(1)}, u32[]{:S(2)}, u32[]{:S(2)}) %collective-permute-start.2) | collective-permute-done | bytes 524320 | tf_op jit(solution)/shard_map/ppermute | solution.py:456
  267.7 7.9 %collective-permute-start.6 = (f32[19,8,128]{2,1,0:T(8,128)S(1)}, f32[19,8,128]{2,1,0:T(8,128)S(1)}, u32[]{:S(2)}, u32[]{:S(2)}) collective-permute-start(f32[19,8,128]{2,1,0:T(8,128)S(1)} %maximum_maximum_fusion), channel_id=1, source_target_pairs={{0,1},{1,2},{2,3},{3,4},{4,5},{5,6},{6,7},{7,8},{8,9},{9,10},{10,1... | collective-permute-start | bytes 233480 | tf_op jit(solution)/shard_map/ppermute | solution.py:512
  275.9 1.2 collective-permute-done.6
  277.1 2.5 collective-permute-done.7
  280.2 153.5 %section.1 = (f32[16,128,512]{2,1,0:T(8,128)}, f32[3,16,128,512]{3,2,1,0:T(8,128)}) custom-call(f32[16,128,512]{2,1,0:T(8,128)} %refs_0_.1, f32[3,16,128,512]{3,2,1,0:T(8,128)} %refs_1_.2, f32[3,16,128,512]{3,2,1,0:T(8,128)} %refs_2_.2, f32[4,16,128,128]{3,2,1,0:T(8,128)} %bitcast.8.refs_3_, f32[6,2,128,512]{3,2,1,0:T(8,128)} %fusion.5.refs_4_, ...), custom_call_target="tpu_custom_call" | custom-call | tf_op jit(solution)/shard_map/section/pallas_call | solution.py:412
  (110 shorter events, 16.4 us)
Async XLA Ops:
  12.8 6.0 %copy-start = (f32[16,128,512]{2,1,0:T(8,128)}, f32[16,128,512]{2,1,0:T(8,128)S(1)}, u32[]{:S(2)}) copy-start(f32[16,128,512]{2,1,0:T(8,128)S(1)} %get-tuple-element.26) | copy-start | bytes 12582916
  12.8 3.7 copy-start.1
  22.5 96.8 %all-to-all-start = ((f32[16,4,128,128]{3,2,1,0:T(8,128)}), f32[16,4,128,128]{3,2,1,0:T(8,128)}, u32[]{:S(2)}, u32[]{:S(2)}) async-start(f32[16,4,128,128]{3,2,1,0:T(8,128)} %bitcast.228), calls=%async_computation | async-start | bytes 8388608 | tf_op jit(solution)/shard_map/all_to_all | solution.py:525
  50.7 1.6 copy-start.4
  52.2 93.9 %collective-permute-start = (f32[11,128,512]{2,1,0:T(8,128)}, f32[11,128,512]{2,1,0:T(8,128)}, u32[]{:S(2)}, u32[]{:S(2)}) collective-permute-start(f32[11,128,512]{2,1,0:T(8,128)} %get-tuple-element.7), channel_id=1, source_target_pairs={{0,16},{1,17},{2,18},{3,19},{4,20},{5,21},{6,22},{7,23},{8,24},{9,... | collective-permute-start | bytes 8650760 | tf_op jit(solution)/shard_map/ppermute | solution.py:456
  53.5 99.4 %collective-permute-start.1 = (f32[12,128,512]{2,1,0:T(8,128)}, f32[12,128,512]{2,1,0:T(8,128)}, u32[]{:S(2)}, u32[]{:S(2)}) collective-permute-start(f32[12,128,512]{2,1,0:T(8,128)} %get-tuple-element.5), channel_id=1, source_target_pairs={{16,0},{17,1},{18,2},{19,3},{20,4},{21,5},{22,6},{23,7},{24,8},{25... | collective-permute-start | bytes 9437192 | tf_op jit(solution)/shard_map/ppermute | solution.py:456
  133.7 103.9 %all-to-all-start.1 = ((f32[16,4,128,128]{3,2,1,0:T(8,128)}), f32[16,4,128,128]{3,2,1,0:T(8,128)}, u32[]{:S(2)}, u32[]{:S(2)}) async-start(f32[16,4,128,128]{3,2,1,0:T(8,128)} %polar_filter.1), calls=%async_computation.1 | async-start | bytes 8388608 | tf_op jit(solution)/shard_map/all_to_all | solution.py:527
  143.4 5.5 %copy-start.2 = (f32[12,128,512]{2,1,0:T(8,128)}, f32[12,128,512]{2,1,0:T(8,128)S(1)}, u32[]{:S(2)}) copy-start(f32[12,128,512]{2,1,0:T(8,128)S(1)} %bitcast_dynamic-update-slice_fusion.3) | copy-start | bytes 9437188
  149.1 3.8 copy-start.6
  149.1 3.8 copy-start.7
  149.1 3.8 copy-start.3
  153.9 6.2 %copy-start.14 = (f32[16,3,512]{2,1,0:T(4,128)S(1)}, f32[16,3,512]{2,1,0:T(4,128)}, u32[]{:S(2)}) copy-start(f32[16,3,512]{2,1,0:T(4,128)} %get-tuple-element.39) | copy-start | bytes 294916
  153.9 7.5 %copy-start.13 = (f32[16,3,512]{2,1,0:T(4,128)S(1)}, f32[16,3,512]{2,1,0:T(4,128)}, u32[]{:S(2)}) copy-start(f32[16,3,512]{2,1,0:T(4,128)} %get-tuple-element.37) | copy-start | bytes 294916
  155.7 5.8 %copy-start.5 = (f32[1,128,512]{2,1,0:T(8,128)}, f32[1,128,512]{2,1,0:T(8,128)S(1)}, u32[]{:S(2)}) copy-start(f32[1,128,512]{2,1,0:T(8,128)S(1)} %get-tuple-element.64) | copy-start | bytes 786436
  177.2 5.2 %copy-start.11 = (f32[1,128,512]{2,1,0:T(8,128)S(1)}, f32[1,128,512]{2,1,0:T(8,128)}, u32[]{:S(2)}) copy-start(f32[1,128,512]{2,1,0:T(8,128)} %get-tuple-element.61) | copy-start | bytes 786436
  177.2 5.2 %copy-start.12 = (f32[1,128,512]{2,1,0:T(8,128)S(1)}, f32[1,128,512]{2,1,0:T(8,128)}, u32[]{:S(2)}) copy-start(f32[1,128,512]{2,1,0:T(8,128)} %get-tuple-element.62) | copy-start | bytes 786436
  177.2 6.1 %copy-start.9 = (f32[1,128,512]{2,1,0:T(8,128)S(1)}, f32[1,128,512]{2,1,0:T(8,128)}, u32[]{:S(2)}) copy-start(f32[1,128,512]{2,1,0:T(8,128)} %get-tuple-element.59) | copy-start | bytes 786436
  177.2 6.1 %copy-start.10 = (f32[1,128,512]{2,1,0:T(8,128)S(1)}, f32[1,128,512]{2,1,0:T(8,128)}, u32[]{:S(2)}) copy-start(f32[1,128,512]{2,1,0:T(8,128)} %get-tuple-element.60) | copy-start | bytes 786436
  177.3 14.3 %collective-permute-start.4 = (f32[19,16,512]{2,1,0:T(8,128)S(1)}, f32[19,16,512]{2,1,0:T(8,128)S(1)}, u32[]{:S(2)}, u32[]{:S(2)}) collective-permute-start(f32[19,16,512]{2,1,0:T(8,128)S(1)} %pad.8), channel_id=1, source_target_pairs={{0,1},{1,2},{2,3},{3,4},{4,5},{5,6},{6,7},{7,8},{8,9},{9,10},{10,1... | collective-permute-start | bytes 1867784 | tf_op jit(solution)/shard_map/ppermute | solution.py:512
  178.8 15.9 %collective-permute-start.5 = (f32[19,16,512]{2,1,0:T(8,128)}, f32[19,16,512]{2,1,0:T(8,128)S(1)}, u32[]{:S(2)}, u32[]{:S(2)}) collective-permute-start(f32[19,16,512]{2,1,0:T(8,128)} %pad.9), channel_id=1, source_target_pairs={{1,0},{2,1},{3,2},{4,3},{5,4},{6,5},{7,6},{8,7},{9,8},{10,9},{11,1... | collective-permute-start | bytes 1867784 | tf_op jit(solution)/shard_map/ppermute | solution.py:512
  240.3 12.4 %collective-permute-start.3 = (f32[8,128,128]{2,1,0:T(8,128)S(1)}, f32[8,128,128]{2,1,0:T(8,128)S(1)}, u32[]{:S(2)}, u32[]{:S(2)}) collective-permute-start(f32[8,128,128]{2,1,0:T(8,128)S(1)} %pad_maximum_fusion.3), channel_id=1, source_target_pairs={{16,0},{17,1},{18,2},{19,3},{20,4},{21,5},{22,6},{23,7},{24,8},{25... | collective-permute-start | bytes 1572872 | tf_op jit(solution)/shard_map/ppermute | solution.py:456
  253.0 13.8 %collective-permute-start.2 = (f32[8,128,128]{2,1,0:T(8,128)S(1)}, f32[8,128,128]{2,1,0:T(8,128)S(1)}, u32[]{:S(2)}, u32[]{:S(2)}) collective-permute-start(f32[8,128,128]{2,1,0:T(8,128)S(1)} %get-tuple-element.146), channel_id=1, source_target_pairs={{0,16},{1,17},{2,18},{3,19},{4,20},{5,21},{6,22},{7,23},{8,24},{9,... | collective-permute-start | bytes 1572872 | tf_op jit(solution)/shard_map/ppermute | solution.py:456
  267.7 9.4 %collective-permute-start.6 = (f32[19,8,128]{2,1,0:T(8,128)S(1)}, f32[19,8,128]{2,1,0:T(8,128)S(1)}, u32[]{:S(2)}, u32[]{:S(2)}) collective-permute-start(f32[19,8,128]{2,1,0:T(8,128)S(1)} %maximum_maximum_fusion), channel_id=1, source_target_pairs={{0,1},{1,2},{2,3},{3,4},{4,5},{5,6},{6,7},{7,8},{8,9},{9,10},{10,1... | collective-permute-start | bytes 233480 | tf_op jit(solution)/shard_map/ppermute | solution.py:512
  275.7 3.9 collective-permute-start.7
  275.9 4.4 %copy-start.8 = (f32[6,2,128,128]{3,2,1,0:T(8,128)}, f32[6,2,128,128]{3,2,1,0:T(8,128)S(1)}, u32[]{:S(2)}) copy-start(f32[6,2,128,128]{3,2,1,0:T(8,128)S(1)} %fusion.9.refs_5_) | copy-start | bytes 2359300
